TPU v7x, 32 devices: a whole 2x2x4 slice. The times are simulated.
32 devices in a mesh: replica: 2 (over x), pipe: 4 (over z), tensor: 4 (over y, core).
Axes of the slice: x: 2, y: 2, z: 4, core: 2. Of those that a mesh axis runs over, the one named last changes fastest.
Arguments:
- queries: bfloat16 [256, 8192], P('replica', ('pipe', 'tensor')), parts along dimension 0, may hold values from -128 to 128, as said below
- cache_keys: bfloat16 [8, 4096, 1024], P('replica', 'tensor', 'pipe'), parts along dimension 0, may hold values from -4 to 4
- cache_values: bfloat16 [8, 4096, 1024], P('replica', 'tensor', 'pipe'), parts along dimension 0, may hold values from -6 to 6
- prefix_lengths: int32 [8], P('replica'), parts along dimension 0, may hold values from 2048 to 4064
- residual_in: bfloat16 [256, 8192], P('replica', ('pipe', 'tensor')), parts along dimension 0, may hold values from -64 to 64
- out_weight: bfloat16 [8192, 4, 2048], P('pipe', None, 'tensor'), may hold values from -0.0625 to 0.0625
- norm_gain: float32 [8192], P(('pipe', 'tensor')), may hold values from 0.1 to 1.9
Outputs:
- residual_out: bfloat16 [256, 8192], P('replica', ('pipe', 'tensor')), parts along dimension 0
- normed: bfloat16 [256, 8192], P('replica', ('pipe', 'tensor')), parts along dimension 0
There are 2 independent parts, one for each index of `replica`. A program takes and returns all parts, laid end to end along the dimension named above; an argument that names none is the same for every part. Nothing has to cross between parts.
Inputs may be any that keep to these rules, and one draw needn't show every extreme that they name: `queries`: entries of the query rows; some rows may be much longer than others. The span's own keys and values already stand in the cache, in slots prefix_lengths[r] to prefix_lengths[r] + 31; later slots hold unused entries.
All inputs are finite; a program needn't handle non-finite values.
Results may differ from a plain program's by a relative error of at most 0.018.
Values may be sent and summed in bfloat16 or wider, within the bound.
A program may use at most 64 MiB of HBM per device.

v0:
```python
import math
import jax
import jax.numpy as jnp
from jax import lax
from jax.sharding import PartitionSpec as P

D = 8192
HD = 128
masked_value = -1e30
epsilon = 1e-05


def combined_all(shard, axis, combine):
    everything = jax.tree.map(
        lambda part, kind: lax.all_gather(part.astype(kind), axis),
        shard,
        (jnp.bfloat16, jnp.bfloat16, jnp.bfloat16),
    )

    def take(k):
        return jax.tree.map(lambda part, own: part[k].astype(own.dtype), everything, shard)

    return lax.fori_loop(
        1, lax.axis_size(axis), lambda k, so_far: combine(so_far, take(k)), take(0)
    )


def combine(first, second):
    peak_one, total_one, summed_one = first
    peak_two, total_two, summed_two = second
    joined = jnp.maximum(peak_one, peak_two)
    factor_one = jnp.exp(peak_one - joined)
    factor_two = jnp.exp(peak_two - joined)
    return (
        joined,
        total_one * factor_one + total_two * factor_two,
        summed_one * factor_one[..., None] + summed_two * factor_two[..., None],
    )


def on_device(
    queries, cache_keys, cache_values, prefix_lengths, residual_in, out_weight, norm_gain
):
    tok_rows = queries.shape[0]
    requests = prefix_lengths.shape[0]
    span_len = tok_rows // requests
    slot_count = cache_keys.shape[1]
    local_groups = cache_keys.shape[2] // HD
    gathered = lax.all_gather(queries, "tensor", axis=1, tiled=True)
    heads_here = gathered.shape[1] // HD
    group_size = heads_here // local_groups
    queries_here = gathered.reshape(requests, span_len, local_groups, group_size, HD)
    keys_here = cache_keys.reshape(requests, slot_count, local_groups, HD)
    values_here = cache_values.reshape(requests, slot_count, local_groups, HD)
    scores = jnp.einsum(
        "rcghd,rjgd->rcghj", queries_here, keys_here, preferred_element_type=jnp.float32
    ) * (1.0 / math.sqrt(HD))
    first_slot = lax.axis_index("tensor") * slot_count
    slot_index = first_slot + jnp.arange(slot_count, dtype=jnp.int32)
    limits = prefix_lengths[:, None] + jnp.arange(span_len, dtype=jnp.int32)[None, :]
    visible = (slot_index[None, None, :] <= limits[:, :, None])[:, :, None, None, :]
    masked = jnp.where(visible, scores, masked_value)
    row_peak = jnp.max(masked, axis=-1)
    weights = jnp.where(visible, jnp.exp(masked - row_peak[..., None]), 0.0)
    row_total = jnp.sum(weights, axis=-1)
    weighted = jnp.einsum(
        "rcghj,rjgd->rcghd",
        weights.astype(jnp.bfloat16),
        values_here,
        preferred_element_type=jnp.float32,
    )
    row_peak = row_peak.reshape(tok_rows, heads_here)
    row_total = row_total.reshape(tok_rows, heads_here)
    weighted = weighted.reshape(tok_rows, heads_here, HD)
    row_peak, row_total, weighted = combined_all((row_peak, row_total, weighted), "tensor", combine)
    attended = (
        (weighted / row_total[..., None]).astype(jnp.bfloat16).reshape(tok_rows, heads_here * HD)
    )
    col_groups = out_weight.shape[1]
    col_width = out_weight.shape[2]
    partial_value = jnp.dot(
        attended,
        out_weight.reshape(out_weight.shape[0], col_groups * col_width),
        preferred_element_type=jnp.float32,
    )
    projected = (
        lax.psum_scatter(
            partial_value.reshape(tok_rows, col_groups, col_width).astype(jnp.bfloat16),
            "pipe",
            scatter_dimension=1,
            tiled=True,
        )
        .astype(jnp.float32)
        .reshape(tok_rows, col_width)
    )
    updated = residual_in.astype(jnp.float32) + projected
    squares = lax.psum(jnp.sum(updated * updated, axis=1), ("pipe", "tensor"))
    normed = updated * lax.rsqrt(squares / D + epsilon)[:, None] * norm_gain[None, :]
    return (updated.astype(jnp.bfloat16), normed.astype(jnp.bfloat16))


def solution(mesh):
    in_specs = (
        P("replica", ("pipe", "tensor")),
        P("replica", "tensor", "pipe"),
        P("replica", "tensor", "pipe"),
        P("replica"),
        P("replica", ("pipe", "tensor")),
        P("pipe", None, "tensor"),
        P(("pipe", "tensor")),
    )
    out_specs = (P("replica", ("pipe", "tensor")), P("replica", ("pipe", "tensor")))
    return jax.shard_map(
        on_device, mesh=mesh, in_specs=in_specs, out_specs=out_specs, check_vma=False
    )
```

profile of v0, /device:TPU:0, one launch (start us, length us, event | category | flops | bytes accessed | tf_op | source)
XLA Modules:
  0.0 146.8 jit_solution(17740853063644884456)
XLA Ops:
  7.2 0.0 all-gather.2.cloned.1.call-start
  7.2 0.7 iota_add_fusion.1
  7.9 8.9 %all_gather.15 = bf16[128,2048]{1,0:T(8,128)(2,1)S(1)} all-gather(bf16[128,512]{1,0:T(8,128)(2,1)} %param.9), channel_id=1, replica_groups=mesh['replica'=2,'pipe'=4,'tensor'=4] {'tensor'}, dimensions={1}, use_global_device_ids=true | all-gather | bytes 655360 | tf_op jit(solution)/shard_map/all_gather | solution.py:49
  16.8 0.1 copy.52
  16.9 4.0 %reshape.107 = bf16[4,1024,2,128]{3,2,1,0:T(2,128)(2,1)} reshape(bf16[4,1024,256]{2,1,0:T(8,128)(2,1)} %param.10) | data formatting | bytes 4194304 | tf_op jit(solution)/shard_map/reshape | solution.py:53
  20.9 2.5 %reshape.109 = bf16[4,1024,2,128]{3,2,1,0:T(2,128)(2,1)S(1)} reshape(bf16[4,1024,256]{2,1,0:T(8,128)(2,1)} %param.11) | data formatting | bytes 4194304 | tf_op jit(solution)/shard_map/reshape | solution.py:54
  23.5 0.1 broadcast_compare_fusion
  23.6 3.3 %fusion.3 = (f32[4,32,2,8]{1,3,2,0:T(8,128)S(1)}, f32[4,2,1024,32,8]{2,3,4,1,0:T(8,128)S(1)}) fusion(pred[4,32,1024]{2,1,0:T(8,128)(4,1)S(1)} %broadcast_compare_fusion, bf16[4,32,2,8,128]{4,3,2,1,0:T(8,128)(2,1)S(1)} %bitcast.77, bf16[4,1024,2,128,1]{3,2,1,0,4:T(2,128)(2,1)} %bitcast.75), kind=kOutput, calls=%fused_computation.10 | convolution fusion | flops 543160320 | bytes 11149312 | tf_op jit(solution)/shard_map/rcghd,rjgd->rcghj/dot_general | solution.py:55
  26.9 0.0 copy-start
  26.9 2.6 %fusion.17 = bf16[4,32,2,8,128]{4,1,3,2,0:T(8,128)(2,1)S(1)} fusion(bf16[4,1024,2,128,1]{3,2,1,0,4:T(2,128)(2,1)S(1)} %bitcast.74, f32[4,2,1024,32,8]{2,3,4,1,0:T(8,128)S(1)} %get-tuple-element.202, f32[4,32,2,8]{1,3,2,0:T(8,128)S(1)} %get-tuple-element.201, pred[4,32,1024]{2,1,0:T(8,128)(4,1)S(1)} %broadcast_compare_fusion), kind=kOutput, calls=%fused_computation.20 | convolution fusion | flops 547618816 | bytes 11149312 | tf_op jit(solution)/shard_map/rcghj,rjgd->rcghd/dot_general | solution.py:66
  29.5 0.6 copy-done
  30.1 1.0 copy.43
  31.1 0.0 all-gather.2.cloned.1.call-update
  31.1 0.0 reduce-scatter.2.cloned.1.call-start
  31.2 0.1 convert_element_type.120
  31.3 4.7 %fusion.5 = bf16[4,32,2,8]{1,3,2,0:T(8,128)(2,1)S(1)} fusion(f32[4,2,1024,32,8]{2,3,4,1,0:T(8,128)} %copy-done, f32[4,32,2,8]{1,3,2,0:T(8,128)S(1)} %get-tuple-element.201, pred[4,32,1024]{2,1,0:T(8,128)(4,1)S(1)} %broadcast_compare_fusion), kind=kLoop, calls=%fused_computation.12 | loop fusion | flops 10483712 | bytes 8531968 | tf_op jit(solution)/shard_map/reduce_sum | solution.py:65
  36.0 0.1 convert_element_type.124
  36.1 10.5 %copy.53 = bf16[256,8,4,512]{3,1,2,0:T(8,128)(2,1)} copy(bf16[256,8,4,512]{3,2,1,0:T(4,128)(2,1)} %bitcast.72) | data formatting | bytes 16777216
  46.6 12.3 %copy.45 = bf16[2048,2048]{1,0:T(8,128)(2,1)} copy(bf16[2048,2048]{0,1:T(8,128)(2,1)} %bitcast.71) | data formatting | bytes 16777216 | tf_op jit(solution)/shard_map/dot_general | solution.py:81
  59.0 5.2 %all_gather.17 = bf16[4,128,16]{1,2,0:T(8,128)(2,1)S(1)} all-gather(bf16[1,128,16]{1,2,0:T(8,128)(2,1)S(1)} %convert_element_type.124), channel_id=1, replica_groups=mesh['replica'=2,'pipe'=4,'tensor'=4] {'tensor'}, dimensions={0}, use_global_device_ids=true | all-gather | bytes 20480 | tf_op jit(solution)/shard_map/all_gather | solution.py:15
  64.2 5.4 %all_gather.16 = bf16[4,128,16]{1,2,0:T(8,128)(2,1)S(1)} all-gather(bf16[1,128,16]{1,2,0:T(8,128)(2,1)S(1)} %convert_element_type.120), channel_id=1, replica_groups=mesh['replica'=2,'pipe'=4,'tensor'=4] {'tensor'}, dimensions={0}, use_global_device_ids=true | all-gather | bytes 20480 | tf_op jit(solution)/shard_map/all_gather | solution.py:15
  69.6 0.0 all-gather.2.cloned.1.call-done
  69.6 1.1 fusion.22
  70.7 6.5 %while.19 = (s32[]{:T(128)}, f32[128,16]{0,1:T(8,128)S(1)}, f32[128,16]{0,1:T(8,128)S(1)}, f32[128,16,128]{2,1,0:T(8,128)S(1)}, bf16[4,128,16]{1,2,0:T(8,128)(2,...) while((s32[]{:T(128)}, f32[128,16]{0,1:T(8,128)S(1)}, ...), condition=%wide.region_3.4_spmd, body=%wide.region_2.3_spmd.sunk | while | flops 1064965 | bytes 2728079 | solution.py:23
  70.7 0.1 copy.70
  70.8 0.1 copy.71
  70.9 1.9 %fusion.36 = f32[128,16,128]{2,1,0:T(8,128)S(1)} fusion(f32[128,16,128]{2,1,0:T(8,128)S(1)} %get-tuple-element.267, f32[128,16]{1,0:T(8,128)S(1)} %copy.70, bf16[4,128,16,128]{3,2,1,0:T(8,128)(2,1)} %get-tuple-element.280, s32[]{:T(128)S(6)} %select_n.46, f32[128,16]{1,0:T(8,128)S(1)} %copy.71), kind=kLoop, calls=%fused_computation.1.clone.1 | loop fusion | flops 1048576 | bytes 2637828 | tf_op jit(solution)/shard_map/while/body/eval_jaxpr/add | solution.py:37
  72.9 0.1 copy.70
  73.0 0.1 copy.71
  73.1 1.9 %fusion.36 = f32[128,16,128]{2,1,0:T(8,128)S(1)} fusion(f32[128,16,128]{2,1,0:T(8,128)S(1)} %get-tuple-element.267, f32[128,16]{1,0:T(8,128)S(1)} %copy.70, bf16[4,128,16,128]{3,2,1,0:T(8,128)(2,1)} %get-tuple-element.280, s32[]{:T(128)S(6)} %select_n.46, f32[128,16]{1,0:T(8,128)S(1)} %copy.71), kind=kLoop, calls=%fused_computation.1.clone.1 | loop fusion | flops 1048576 | bytes 2637828 | tf_op jit(solution)/shard_map/while/body/eval_jaxpr/add | solution.py:37
  75.1 0.1 copy.70
  75.2 0.1 copy.71
  75.3 1.9 %fusion.36 = f32[128,16,128]{2,1,0:T(8,128)S(1)} fusion(f32[128,16,128]{2,1,0:T(8,128)S(1)} %get-tuple-element.267, f32[128,16]{1,0:T(8,128)S(1)} %copy.70, bf16[4,128,16,128]{3,2,1,0:T(8,128)(2,1)} %get-tuple-element.280, s32[]{:T(128)S(6)} %select_n.46, f32[128,16]{1,0:T(8,128)S(1)} %copy.71), kind=kLoop, calls=%fused_computation.1.clone.1 | loop fusion | flops 1048576 | bytes 2637828 | tf_op jit(solution)/shard_map/while/body/eval_jaxpr/add | solution.py:37
  77.2 0.0 copy-start.1
  77.2 0.0 copy-start.2
  77.3 0.1 copy.44
  77.4 0.3 divide_convert_fusion
  77.7 0.2 reshape.124
  77.9 7.1 %convolution_convert_fusion = bf16[128,4,512]{2,0,1:T(8,128)(2,1)} fusion(bf16[128,2048,1]{1,0,2:T(8,128)(2,1)S(1)} %reshape.124, bf16[4,512,2048]{2,1,0:T(8,128)(2,1)} %bitcast.70), kind=kOutput, calls=%fused_computation.19 | convolution fusion | flops 1074003968 | bytes 9437184 | tf_op jit(solution)/shard_map/dot_general | solution.py:81
  85.1 0.0 reduce-scatter.2.cloned.1.call-update
  85.1 22.6 %reduce-scatter.2.cloned.1.call-done = bf16[128,1,512]{2,0,1:T(8,128)(2,1)} async-done(((bf16[128,4,512]{2,0,1:T(8,128)(2,1)}), bf16[128,1,512]{2,0,1:T(8,128)(2,1)}) %reduce-scatter.2.cloned.1.call-update) | async-done | bytes 131088 | tf_op jit(solution)/shard_map/reduce_scatter | solution.py:87
  107.7 0.0 copy-done.1
  107.7 1.0 multiply_reduce_fusion
  108.8 29.5 %psum.7 = f32[128]{0:T(128)S(1)} all-reduce(f32[128]{0:T(128)S(1)} %multiply_reduce_fusion), channel_id=1, replica_groups=mesh['replica'=2,'pipe'=4,'tensor'=4] {'pipe','tensor'}, use_global_device_ids=true, to_apply=%region_6.7 | all-reduce | flops 128 | bytes 1024 | tf_op jit(solution)/shard_map/psum | solution.py:97
  138.3 0.0 copy-done.2
  138.3 1.7 %multiply_convert_fusion = (bf16[128,512]{1,0:T(8,128)(2,1)}, bf16[128,512]{1,0:T(8,128)(2,1)}) fusion(bf16[128,512]{1,0:T(8,128)(2,1)S(1)} %copy-done.1, bf16[128,1,512]{2,0,1:T(8,128)(2,1)} %reduce-scatter.2.cloned.1.call-done, f32[512]{0:T(512)S(1)} %copy-done.2, f32[128]{0:T(128)S(1)} %add_rsqrt_fusion), kind=kLoop, calls=%fused_computation.26 | loop fusion | flops 458752 | bytes 526848 | tf_op jit(solution)/shard_map/convert_element_type | solution.py:99
  (10 shorter events, 0.1 us)
Async XLA Ops:
  7.2 62.4 %all-gather.2.cloned.1.call-start = ((), (), s32[]{:S(2)}) async-start(), calls=%async_computation.1 | async-start | bytes 2621440 | tf_op jit(solution)/shard_map/all_gather | solution.py:15
  26.9 3.2 %copy-start = (f32[4,2,1024,32,8]{2,3,4,1,0:T(8,128)}, f32[4,2,1024,32,8]{2,3,4,1,0:T(8,128)S(1)}, u32[]{:S(2)}) copy-start(f32[4,2,1024,32,8]{2,3,4,1,0:T(8,128)S(1)} %get-tuple-element.202) | copy-start | bytes 25165828
  31.1 76.6 %reduce-scatter.2.cloned.1.call-start = ((), (), s32[]{:S(2)}) async-start(), calls=%async_computation.2 | async-start | bytes 655360 | tf_op jit(solution)/shard_map/reduce_scatter | solution.py:87
  77.2 30.5 %copy-start.1 = (bf16[128,512]{1,0:T(8,128)(2,1)S(1)}, bf16[128,512]{1,0:T(8,128)(2,1)}, u32[]{:S(2)}) copy-start(bf16[128,512]{1,0:T(8,128)(2,1)} %param.13) | copy-start | bytes 393220
  77.2 61.0 %copy-start.2 = (f32[512]{0:T(512)S(1)}, f32[512]{0:T(512)}, u32[]{:S(2)}) copy-start(f32[512]{0:T(512)} %param.15) | copy-start | bytes 6148
Sparse Core Ops, SparseCore 0:
  31.2 23.3 all-gather.1
  85.2 22.4 reduce-scatter.1
where the time goes:
time: 148 us; the launch traced here: 147 us
  blocking collectives  48.9 us (33%)
  local copies, waits for them, and re-layouts  32.2 us (22%)
  waiting for transfers between devices  22.7 us (15%)
  other arithmetic  15.6 us (11%)
  between operations  14.2 us (10%)
  matrix products  13 us (9%)
    psum x1, blocking collectives, on_device(): squares = lax.psum(jnp.sum(updated * updated, axis=1), ('pipe', 'tensor'))  29.5 us
    reduce_scatter x1, waiting for transfers between devices, on_device(): lax.psum_scatter(partial_value.reshape(tok_rows, col_groups, col_width).a...  22.6 us
    dot_general x1, local copies, waits for them, and re-layouts, on_device(): jnp.dot(attended, out_weight.reshape(out_weight.shape[0], col_groups * co...  12.3 us
    unnamed x8, local copies, waits for them, and re-layouts  11.2 us
    all_gather x2, blocking collectives, combined_all(): lax.all_gather(part.astype(kind), axis)  10.6 us
    all_gather x1, blocking collectives, on_device(): gathered = lax.all_gather(queries, 'tensor', axis=1, tiled=True)  8.87 us
    dot_general x1, matrix products, on_device(): jnp.dot(attended, out_weight.reshape(out_weight.shape[0], col_groups * co...  7.12 us
    add x3, other arithmetic, combine(): summed_one * factor_one[..., None] + summed_two * factor_two[..., None]  5.79 us
  transfers between devices with their start and end apart: 2, of which 1 were waited for; matrix products, arithmetic and copies ran while one was open for 19% of the time, Pallas kernels for 0%

commit v1 on v0

--- a/solution.py
+++ b/solution.py
@@ -94,7 +94,9 @@
         .reshape(tok_rows, col_width)
     )
     updated = residual_in.astype(jnp.float32) + projected
-    squares = lax.psum(jnp.sum(updated * updated, axis=1), ("pipe", "tensor"))
+    squares = jnp.sum(
+        lax.all_gather(jnp.sum(updated * updated, axis=1), ("pipe", "tensor")), axis=0
+    )
     normed = updated * lax.rsqrt(squares / D + epsilon)[:, None] * norm_gain[None, :]
     return (updated.astype(jnp.bfloat16), normed.astype(jnp.bfloat16))
 

time: 148 us -> 137 us (0.926)
  blocking collectives: 48.9 us -> 38 us
    psum x1 -> x0, blocking collectives: 29.5 us -> none  [on_device(): squares = lax.psum(jnp.sum(updated * updated, axis=1), ('pipe', 'tensor'))]
    all_gather x0 -> x1, blocking collectives: none -> 18.5 us  [on_device(): lax.all_gather(jnp.sum(updated * updated, axis=1), ('pipe', 'tensor'))]
  transfers between devices with their start and end apart: 2 -> 2, of which waited for: 1 -> 1; matrix products, arithmetic and copies ran while one was open for 19% -> 20% of each run, Pallas kernels for 0% -> 0%
where the time goes in v1:
time: 137 us; the launch traced here: 136 us
  blocking collectives  38 us (28%)
  local copies, waits for them, and re-layouts  32.2 us (24%)
  waiting for transfers between devices  22.7 us (17%)
  other arithmetic  15.6 us (11%)
  between operations  14.2 us (10%)
  matrix products  13 us (9%)
    reduce_scatter x1, waiting for transfers between devices, on_device(): lax.psum_scatter(partial_value.reshape(tok_rows, col_groups, col_width).a...  22.6 us
    all_gather x1, blocking collectives, on_device(): lax.all_gather(jnp.sum(updated * updated, axis=1), ('pipe', 'tensor'))  18.5 us
    dot_general x1, local copies, waits for them, and re-layouts, on_device(): jnp.dot(attended, out_weight.reshape(out_weight.shape[0], col_groups * co...  12.3 us
    unnamed x8, local copies, waits for them, and re-layouts  11.2 us
    all_gather x2, blocking collectives, combined_all(): lax.all_gather(part.astype(kind), axis)  10.6 us
    all_gather x1, blocking collectives, on_device(): gathered = lax.all_gather(queries, 'tensor', axis=1, tiled=True)  8.87 us
    dot_general x1, matrix products, on_device(): jnp.dot(attended, out_weight.reshape(out_weight.shape[0], col_groups * co...  7.12 us
    add x3, other arithmetic, combine(): summed_one * factor_one[..., None] + summed_two * factor_two[..., None]  5.79 us
  transfers between devices with their start and end apart: 2, of which 1 were waited for; matrix products, arithmetic and copies ran while one was open for 20% of the time, Pallas kernels for 0%

profile of v1, /device:TPU:0, one launch (start us, length us, event | category | flops | bytes accessed | tf_op | source)
XLA Modules:
  0.0 135.8 jit_solution(6000921724019364861)
XLA Ops:
  7.2 0.0 all-gather.4.cloned.1.call-start
  7.2 0.7 iota_add_fusion.1
  7.9 8.9 %all_gather.21 = bf16[128,2048]{1,0:T(8,128)(2,1)S(1)} all-gather(bf16[128,512]{1,0:T(8,128)(2,1)} %param.9), channel_id=1, replica_groups=mesh['replica'=2,'pipe'=4,'tensor'=4] {'tensor'}, dimensions={1}, use_global_device_ids=true | all-gather | bytes 655360 | tf_op jit(solution)/shard_map/all_gather | solution.py:49
  16.8 0.1 copy.52
  16.9 4.0 %reshape.111 = bf16[4,1024,2,128]{3,2,1,0:T(2,128)(2,1)} reshape(bf16[4,1024,256]{2,1,0:T(8,128)(2,1)} %param.10) | data formatting | bytes 4194304 | tf_op jit(solution)/shard_map/reshape | solution.py:53
  20.9 2.5 %reshape.113 = bf16[4,1024,2,128]{3,2,1,0:T(2,128)(2,1)S(1)} reshape(bf16[4,1024,256]{2,1,0:T(8,128)(2,1)} %param.11) | data formatting | bytes 4194304 | tf_op jit(solution)/shard_map/reshape | solution.py:54
  23.5 0.1 broadcast_compare_fusion
  23.6 3.3 %fusion.3 = (f32[4,32,2,8]{1,3,2,0:T(8,128)S(1)}, f32[4,2,1024,32,8]{2,3,4,1,0:T(8,128)S(1)}) fusion(pred[4,32,1024]{2,1,0:T(8,128)(4,1)S(1)} %broadcast_compare_fusion, bf16[4,32,2,8,128]{4,3,2,1,0:T(8,128)(2,1)S(1)} %bitcast.78, bf16[4,1024,2,128,1]{3,2,1,0,4:T(2,128)(2,1)} %bitcast.76), kind=kOutput, calls=%fused_computation.10 | convolution fusion | flops 543160320 | bytes 11149312 | tf_op jit(solution)/shard_map/rcghd,rjgd->rcghj/dot_general | solution.py:55
  26.9 0.0 copy-start
  26.9 2.6 %fusion.17 = bf16[4,32,2,8,128]{4,1,3,2,0:T(8,128)(2,1)S(1)} fusion(bf16[4,1024,2,128,1]{3,2,1,0,4:T(2,128)(2,1)S(1)} %bitcast.75, f32[4,2,1024,32,8]{2,3,4,1,0:T(8,128)S(1)} %get-tuple-element.202, f32[4,32,2,8]{1,3,2,0:T(8,128)S(1)} %get-tuple-element.201, pred[4,32,1024]{2,1,0:T(8,128)(4,1)S(1)} %broadcast_compare_fusion), kind=kOutput, calls=%fused_computation.20 | convolution fusion | flops 547618816 | bytes 11149312 | tf_op jit(solution)/shard_map/rcghj,rjgd->rcghd/dot_general | solution.py:66
  29.5 0.6 copy-done
  30.1 1.0 copy.43
  31.1 0.0 all-gather.4.cloned.1.call-update
  31.1 0.0 reduce-scatter.2.cloned.1.call-start
  31.2 0.1 convert_element_type.120
  31.3 4.7 %fusion.5 = bf16[4,32,2,8]{1,3,2,0:T(8,128)(2,1)S(1)} fusion(f32[4,2,1024,32,8]{2,3,4,1,0:T(8,128)} %copy-done, f32[4,32,2,8]{1,3,2,0:T(8,128)S(1)} %get-tuple-element.201, pred[4,32,1024]{2,1,0:T(8,128)(4,1)S(1)} %broadcast_compare_fusion), kind=kLoop, calls=%fused_computation.12 | loop fusion | flops 10483712 | bytes 8531968 | tf_op jit(solution)/shard_map/reduce_sum | solution.py:65
  36.0 0.1 convert_element_type.124
  36.1 10.5 %copy.53 = bf16[256,8,4,512]{3,1,2,0:T(8,128)(2,1)} copy(bf16[256,8,4,512]{3,2,1,0:T(4,128)(2,1)} %bitcast.73) | data formatting | bytes 16777216
  46.6 12.3 %copy.45 = bf16[2048,2048]{1,0:T(8,128)(2,1)} copy(bf16[2048,2048]{0,1:T(8,128)(2,1)} %bitcast.72) | data formatting | bytes 16777216 | tf_op jit(solution)/shard_map/dot_general | solution.py:81
  59.0 5.2 %all_gather.23 = bf16[4,128,16]{1,2,0:T(8,128)(2,1)S(1)} all-gather(bf16[1,128,16]{1,2,0:T(8,128)(2,1)S(1)} %convert_element_type.124), channel_id=1, replica_groups=mesh['replica'=2,'pipe'=4,'tensor'=4] {'tensor'}, dimensions={0}, use_global_device_ids=true | all-gather | bytes 20480 | tf_op jit(solution)/shard_map/all_gather | solution.py:15
  64.2 5.4 %all_gather.22 = bf16[4,128,16]{1,2,0:T(8,128)(2,1)S(1)} all-gather(bf16[1,128,16]{1,2,0:T(8,128)(2,1)S(1)} %convert_element_type.120), channel_id=1, replica_groups=mesh['replica'=2,'pipe'=4,'tensor'=4] {'tensor'}, dimensions={0}, use_global_device_ids=true | all-gather | bytes 20480 | tf_op jit(solution)/shard_map/all_gather | solution.py:15
  69.6 0.0 all-gather.4.cloned.1.call-done
  69.6 1.1 fusion.22
  70.7 6.5 %while.19 = (s32[]{:T(128)}, f32[128,16]{0,1:T(8,128)S(1)}, f32[128,16]{0,1:T(8,128)S(1)}, f32[128,16,128]{2,1,0:T(8,128)S(1)}, bf16[4,128,16]{1,2,0:T(8,128)(2,...) while((s32[]{:T(128)}, f32[128,16]{0,1:T(8,128)S(1)}, ...), condition=%wide.region_3.4_spmd, body=%wide.region_2.3_spmd.sunk | while | flops 1064965 | bytes 2728079 | solution.py:23
  70.7 0.1 copy.70
  70.8 0.1 copy.71
  70.9 1.9 %fusion.36 = f32[128,16,128]{2,1,0:T(8,128)S(1)} fusion(f32[128,16,128]{2,1,0:T(8,128)S(1)} %get-tuple-element.267, f32[128,16]{1,0:T(8,128)S(1)} %copy.70, bf16[4,128,16,128]{3,2,1,0:T(8,128)(2,1)} %get-tuple-element.280, s32[]{:T(128)S(6)} %select_n.46, f32[128,16]{1,0:T(8,128)S(1)} %copy.71), kind=kLoop, calls=%fused_computation.1.clone.1 | loop fusion | flops 1048576 | bytes 2637828 | tf_op jit(solution)/shard_map/while/body/eval_jaxpr/add | solution.py:37
  72.9 0.1 copy.70
  73.0 0.1 copy.71
  73.1 1.9 %fusion.36 = f32[128,16,128]{2,1,0:T(8,128)S(1)} fusion(f32[128,16,128]{2,1,0:T(8,128)S(1)} %get-tuple-element.267, f32[128,16]{1,0:T(8,128)S(1)} %copy.70, bf16[4,128,16,128]{3,2,1,0:T(8,128)(2,1)} %get-tuple-element.280, s32[]{:T(128)S(6)} %select_n.46, f32[128,16]{1,0:T(8,128)S(1)} %copy.71), kind=kLoop, calls=%fused_computation.1.clone.1 | loop fusion | flops 1048576 | bytes 2637828 | tf_op jit(solution)/shard_map/while/body/eval_jaxpr/add | solution.py:37
  75.1 0.1 copy.70
  75.2 0.1 copy.71
  75.3 1.9 %fusion.36 = f32[128,16,128]{2,1,0:T(8,128)S(1)} fusion(f32[128,16,128]{2,1,0:T(8,128)S(1)} %get-tuple-element.267, f32[128,16]{1,0:T(8,128)S(1)} %copy.70, bf16[4,128,16,128]{3,2,1,0:T(8,128)(2,1)} %get-tuple-element.280, s32[]{:T(128)S(6)} %select_n.46, f32[128,16]{1,0:T(8,128)S(1)} %copy.71), kind=kLoop, calls=%fused_computation.1.clone.1 | loop fusion | flops 1048576 | bytes 2637828 | tf_op jit(solution)/shard_map/while/body/eval_jaxpr/add | solution.py:37
  77.2 0.0 copy-start.1
  77.2 0.0 copy-start.2
  77.3 0.1 copy.44
  77.4 0.3 divide_convert_fusion
  77.7 0.2 reshape.132
  77.9 7.1 %convolution_convert_fusion = bf16[128,4,512]{2,0,1:T(8,128)(2,1)} fusion(bf16[128,2048,1]{1,0,2:T(8,128)(2,1)S(1)} %reshape.132, bf16[4,512,2048]{2,1,0:T(8,128)(2,1)} %bitcast.71), kind=kOutput, calls=%fused_computation.19 | convolution fusion | flops 1074003968 | bytes 9437184 | tf_op jit(solution)/shard_map/dot_general | solution.py:81
  85.1 0.0 reduce-scatter.2.cloned.1.call-update
  85.1 22.6 %reduce-scatter.2.cloned.1.call-done = bf16[128,1,512]{2,0,1:T(8,128)(2,1)} async-done(((bf16[128,4,512]{2,0,1:T(8,128)(2,1)}), bf16[128,1,512]{2,0,1:T(8,128)(2,1)}) %reduce-scatter.2.cloned.1.call-update) | async-done | bytes 131088 | tf_op jit(solution)/shard_map/reduce_scatter | solution.py:87
  107.7 0.0 copy-done.1
  107.7 1.0 multiply_reduce_fusion
  108.8 18.5 %all-gather.1 = f32[16,1,128]{2,1,0:T(1,128)S(1)} all-gather(f32[1,1,128]{2,1,0:T(1,128)S(1)} %bitcast.79), channel_id=2, replica_groups=mesh['replica'=2,'pipe'=4,'tensor'=4] {'pipe','tensor'}, dimensions={0}, use_global_device_ids=true | all-gather | bytes 8704 | tf_op jit(solution)/shard_map/all_gather | solution.py:98
  127.3 0.0 copy-done.2
  127.3 1.7 %multiply_convert_fusion = (bf16[128,512]{1,0:T(8,128)(2,1)}, bf16[128,512]{1,0:T(8,128)(2,1)}) fusion(bf16[128,512]{1,0:T(8,128)(2,1)S(1)} %copy-done.1, bf16[128,1,512]{2,0,1:T(8,128)(2,1)} %reduce-scatter.2.cloned.1.call-done, f32[512]{0:T(512)S(1)} %copy-done.2, f32[128]{0:T(128)S(1)} %add_rsqrt_fusion), kind=kLoop, calls=%fused_computation.26 | loop fusion | flops 458752 | bytes 526848 | tf_op jit(solution)/shard_map/convert_element_type | solution.py:101
  (11 shorter events, 0.1 us)
Async XLA Ops:
  7.2 62.4 %all-gather.4.cloned.1.call-start = ((), (), s32[]{:S(2)}) async-start(), calls=%async_computation.1 | async-start | bytes 2621440 | tf_op jit(solution)/shard_map/all_gather | solution.py:15
  26.9 3.2 %copy-start = (f32[4,2,1024,32,8]{2,3,4,1,0:T(8,128)}, f32[4,2,1024,32,8]{2,3,4,1,0:T(8,128)S(1)}, u32[]{:S(2)}) copy-start(f32[4,2,1024,32,8]{2,3,4,1,0:T(8,128)S(1)} %get-tuple-element.202) | copy-start | bytes 25165828
  31.1 76.6 %reduce-scatter.2.cloned.1.call-start = ((), (), s32[]{:S(2)}) async-start(), calls=%async_computation.2 | async-start | bytes 655360 | tf_op jit(solution)/shard_map/reduce_scatter | solution.py:87
  77.2 30.5 %copy-start.1 = (bf16[128,512]{1,0:T(8,128)(2,1)S(1)}, bf16[128,512]{1,0:T(8,128)(2,1)}, u32[]{:S(2)}) copy-start(bf16[128,512]{1,0:T(8,128)(2,1)} %param.13) | copy-start | bytes 393220
  77.2 50.1 %copy-start.2 = (f32[512]{0:T(512)S(1)}, f32[512]{0:T(512)}, u32[]{:S(2)}) copy-start(f32[512]{0:T(512)} %param.15) | copy-start | bytes 6148
Sparse Core Ops, SparseCore 0:
  31.2 23.3 all-gather.3
  85.2 22.4 reduce-scatter.1
